TPU v7x, 32 devices: a whole 2x2x4 slice. The times are simulated.
32 devices in a mesh: dp: 4 (over z), sx: 4 (over y, core), sy: 2 (over x).
Axes of the slice: x: 2, y: 2, z: 4, core: 2. Of those that a mesh axis runs over, the one named last changes fastest.
Arguments:
- volume: bfloat16 [4, 4, 16, 16, 128], P('dp', None, 'sx', 'sy'), may hold values from -6 to 6
- first_weight: bfloat16 [32, 108], replicated, may hold values from -0.625 to 0.625
- second_weight: bfloat16 [64, 864], replicated, may hold values from -0.21875 to 0.21875
- cotangent: bfloat16 [4, 64, 8, 8, 64], P('dp', None, 'sx', 'sy'), may hold values from -6 to 6
Outputs:
- grad_first: float32 [32, 108], replicated
- grad_second: float32 [64, 864], replicated
All inputs are finite; a program needn't handle non-finite values.
Results may differ from a plain program's by a relative error of at most 0.014.
Values may be sent and summed in bfloat16 or wider, within the bound.
A program may use at most 64 MiB of HBM per device.

v0:
```python
import jax
import jax.numpy as jnp
from jax import lax
from jax.sharding import PartitionSpec as P


def padded_2(block, sides, width):
    for axis, dim in sides:
        count = lax.axis_size(axis)
        forward = [(i, i + 1) for i in range(count - 1)]
        backward = [(target, source) for source, target in forward]
        low = lax.ppermute(
            lax.slice_in_dim(block, block.shape[dim] - width, None, axis=dim), axis, forward
        )
        high = lax.ppermute(lax.slice_in_dim(block, 0, width, axis=dim), axis, backward)
        block = jnp.concatenate([low, block, high], axis=dim)
    return block


def leaky(value):
    return 0.3 * value + 0.7 * jax.nn.softplus(value)


def slope(value):
    return 0.3 + 0.7 * jax.nn.sigmoid(value)


def patches(padded, width_x, width_y, width_z):
    columns = []
    for shift_x in range(3):
        for shift_y in range(3):
            for shift_z in range(3):
                columns.append(
                    padded[
                        :,
                        shift_x : shift_x + width_x,
                        shift_y : shift_y + width_y,
                        shift_z : shift_z + width_z,
                    ]
                )
    stacked = jnp.concatenate(columns, 0)
    return stacked.reshape(stacked.shape[0], width_x * width_y * width_z)


def pad_depth(field):
    return jnp.pad(field, ((0, 0), (0, 0), (0, 0), (1, 1)))


def shards(volume, first_weight, second_weight, cotangent):
    sample = volume[0]
    chans, width_x, width_y, width_z = sample.shape
    devices = lax.axis_size("dp") * lax.axis_size("sx") * lax.axis_size("sy")
    fine_rim = padded_2(sample, (("sx", 1), ("sy", 2)), 1)
    fine_cols = patches(pad_depth(fine_rim), width_x, width_y, width_z)
    pre_first = jnp.dot(first_weight, fine_cols, preferred_element_type=jnp.float32)
    hidden = leaky(pre_first).astype(jnp.bfloat16)
    inner = hidden.shape[0]
    half_x, half_y, half_z = (width_x // 2, width_y // 2, width_z // 2)
    pooled = (
        hidden.astype(jnp.float32)
        .reshape(inner, half_x, 2, half_y, 2, half_z, 2)
        .sum(axis=(2, 4, 6))
        * 0.125
    ).astype(jnp.bfloat16)
    pooled_rim = padded_2(pooled, (("sx", 1), ("sy", 2)), 1)
    coarse_cols = patches(pad_depth(pooled_rim), half_x, half_y, half_z)
    pre_second = jnp.dot(second_weight, coarse_cols, preferred_element_type=jnp.float32)
    outer = pre_second.shape[0]
    back = (cotangent[0].reshape(outer, -1).astype(jnp.float32) * slope(pre_second)).astype(
        jnp.bfloat16
    )
    coarse_count = half_x * half_y * half_z * devices
    scale_second = 1.0 / jnp.sqrt(jnp.float32(coarse_count))
    scale_first = 1.0 / jnp.sqrt(jnp.float32(coarse_count * 8))
    grad_second = (
        lax.dot_general(
            back, coarse_cols, (((1,), (1,)), ((), ())), preferred_element_type=jnp.float32
        )
        * scale_second
    )
    back_rim = padded_2(back.reshape(outer, half_x, half_y, half_z), (("sx", 1), ("sy", 2)), 1)
    back_cols = patches(pad_depth(back_rim), half_x, half_y, half_z)
    mirrored = (
        second_weight.reshape(outer, 27, inner)[:, ::-1, :]
        .transpose(2, 1, 0)
        .reshape(inner, 27 * outer)
    )
    up = jnp.dot(mirrored, back_cols, preferred_element_type=jnp.float32)
    spread = jnp.broadcast_to(
        up.reshape(inner, half_x, 1, half_y, 1, half_z, 1), (inner, half_x, 2, half_y, 2, half_z, 2)
    ).reshape(inner, -1)
    lower = (spread * 0.125 * slope(pre_first)).astype(jnp.bfloat16)
    grad_first = (
        lax.dot_general(
            lower, fine_cols, (((1,), (1,)), ((), ())), preferred_element_type=jnp.float32
        )
        * scale_first
    )
    shared = (
        lax.psum_scatter(
            grad_first.astype(jnp.bfloat16), ("sx", "sy"), scatter_dimension=0, tiled=True
        ).astype(jnp.float32),
        lax.psum_scatter(
            grad_second.astype(jnp.bfloat16), ("sx", "sy"), scatter_dimension=0, tiled=True
        ).astype(jnp.float32),
    )
    shared = lax.psum((shared[0], shared[1]), "dp")
    grad_first, grad_second = (
        lax.all_gather(shared[0], ("sx", "sy"), axis=0, tiled=True),
        lax.all_gather(shared[1], ("sx", "sy"), axis=0, tiled=True),
    )
    return (grad_first, grad_second)


def solution(mesh):
    return jax.shard_map(
        shards,
        mesh=mesh,
        in_specs=(P("dp", None, "sx", "sy", None), P(), P(), P("dp", None, "sx", "sy", None)),
        out_specs=(P(), P()),
        check_vma=False,
    )
```

profile of v0, /device:TPU:0, one launch (start us, length us, event | category | flops | bytes accessed | tf_op | source)
XLA Modules:
  0.0 207.3 jit_solution(6749969575583011790)
XLA Ops:
  8.0 2.4 %collective-permute-start = (bf16[4,1,8,128]{3,2,1,0:T(8,128)(2,1)S(1)}, bf16[4,1,8,128]{3,2,1,0:T(8,128)(2,1)S(1)}, u32[]{:S(2)}, u32[]{:S(2)}) collective-permute-start(bf16[4,1,8,128]{3,2,1,0:T(8,128)(2,1)S(1)} %get-tuple-element.100), channel_id=1, source_target_pairs={{0,2},{2,4},{4,6},{1,3},{3,5},{5,7},{8,10},{10,12},{12,14},{9,11},... | collective-permute-start | bytes 24584 | tf_op jit(solution)/shard_map/ppermute | solution.py:12
  10.3 1.3 collective-permute-start.1
  11.6 0.8 concatenate.201
  12.4 1.1 copy.12
  13.5 2.0 collective-permute-done.1
  15.5 0.9 pad_maximum_fusion.19
  16.4 3.4 %collective-permute-start.2 = (bf16[4,6,1,128]{3,2,1,0:T(2,128)(2,1)S(1)}, bf16[4,6,1,128]{3,2,1,0:T(2,128)(2,1)S(1)}, u32[]{:S(2)}, u32[]{:S(2)}) collective-permute-start(bf16[4,6,1,128]{3,2,1,0:T(2,128)(2,1)S(1)} %get-tuple-element.96), channel_id=1, source_target_pairs={{0,1},{2,3},{4,5},{6,7},{8,9},{10,11},{12,13},{14,15},{16,17},{18,... | collective-permute-start | bytes 18440 | tf_op jit(solution)/shard_map/ppermute | solution.py:12
  19.8 1.3 collective-permute-start.3
  21.1 0.8 fusion.36
  22.0 3.4 %collective-permute-done.3 = bf16[4,6,1,128]{3,2,1,0:T(2,128)(2,1)S(1)} collective-permute-done((bf16[4,6,1,128]{3,2,1,0:T(2,128)(2,1)S(1)}, bf16[4,6,1,128]{3,2,1,0:T(2,128)(2,1)S(1)}, u32[]{:S(2)}, u32[]{:S(2)}) %collective-permute-start.3) | collective-permute-done | bytes 6176 | tf_op jit(solution)/shard_map/ppermute | solution.py:15
  25.4 0.9 pad_maximum_fusion.11
  27.9 1.4 fusion.27
  29.3 1.6 copy.11
  31.0 1.3 reduce_sum.9
  32.4 2.9 %collective-permute-start.4 = (bf16[32,1,4,64]{0,3,2,1:T(8,128)(2,1)S(1)}, bf16[32,1,4,64]{0,3,2,1:T(8,128)(2,1)S(1)}, u32[]{:S(2)}, u32[]{:S(2)}) collective-permute-start(bf16[32,1,4,64]{0,3,2,1:T(8,128)(2,1)S(1)} %get-tuple-element.86), channel_id=1, source_target_pairs={{0,2},{2,4},{4,6},{1,3},{3,5},{5,7},{8,10},{10,12},{12,14},{9,11},... | collective-permute-start | bytes 49160 | tf_op jit(solution)/shard_map/ppermute | solution.py:12
  35.3 1.3 collective-permute-start.5
  38.5 1.7 reshape.95
  40.3 0.9 reshape.94
  41.2 2.0 collective-permute-start.6
  43.2 1.3 collective-permute-start.7
  45.3 4.1 %collective-permute-done.7 = bf16[32,4,1,64]{0,3,2,1:T(8,128)(2,1)S(1)} collective-permute-done((bf16[32,4,1,64]{0,3,2,1:T(8,128)(2,1)S(1)}, bf16[32,4,1,64]{0,3,2,1:T(8,128)(2,1)S(1)}, u32[]{:S(2)}, u32[]{:S(2)}) %collective-permute-start.7) | collective-permute-done | bytes 16416 | tf_op jit(solution)/shard_map/ppermute | solution.py:15
  49.5 0.8 fusion.43
  50.3 0.8 fusion.44
  51.3 1.1 fusion.42
  52.4 4.9 %concatenate.223 = bf16[864,2,4,64]{0,3,2,1:T(8,128)(2,1)S(1)} concatenate(bf16[32,2,4,64]{0,3,2,1:T(8,128)(2,1)} %get-tuple-element.39, bf16[32,2,4,64]{0,3,2,1:T(8,128)(2,1)} %get-tuple-element.51, bf16[32,2,4,64]{0,3,2,1:T(8,128)(2,1)} %get-tuple-element.38, bf16[32,2,4,64]{0,3,2,1:T(8,128)(2,1)} %get-tuple-element.37, bf16[32,2,4,64]{0,3,2,1:T(8,128)(2,1)} %get-tuple-element.85, ...), dimensions={0} | concatenate | bytes 1769472 | tf_op jit(solution)/shard_map/concatenate | solution.py:41
  57.3 1.4 fusion.8
  58.9 2.7 %collective-permute-start.8 = (bf16[64,1,4,64]{3,2,1,0:T(4,128)(2,1)S(1)}, bf16[64,1,4,64]{3,2,1,0:T(4,128)(2,1)S(1)}, u32[]{:S(2)}, u32[]{:S(2)}) collective-permute-start(bf16[64,1,4,64]{3,2,1,0:T(4,128)(2,1)S(1)} %get-tuple-element.83), channel_id=1, source_target_pairs={{0,2},{2,4},{4,6},{1,3},{3,5},{5,7},{8,10},{10,12},{12,14},{9,11},... | collective-permute-start | bytes 98312 | tf_op jit(solution)/shard_map/ppermute | solution.py:12
  61.6 0.9 fusion
  62.6 1.3 collective-permute-start.9
  63.9 4.5 %collective-permute-done.9 = bf16[64,1,4,64]{3,2,1,0:T(4,128)(2,1)S(1)} collective-permute-done((bf16[64,1,4,64]{3,2,1,0:T(4,128)(2,1)S(1)}, bf16[64,1,4,64]{3,2,1,0:T(4,128)(2,1)S(1)}, u32[]{:S(2)}, u32[]{:S(2)}) %collective-permute-start.9) | collective-permute-done | bytes 32800 | tf_op jit(solution)/shard_map/ppermute | solution.py:15
  69.0 0.8 concatenate.232
  69.8 1.6 collective-permute-start.10
  71.4 1.5 collective-permute-start.11
  72.8 44.2 %all-reduce.8.cloned.1.call-done = bf16[64,864]{1,0:T(8,128)(2,1)} async-done(((bf16[64,864]{1,0:T(8,128)(2,1)}), bf16[64,864]{1,0:T(8,128)(2,1)}) %all-reduce.8.cloned.1.call-update) | async-done | bytes 110608
  117.8 1.1 pad_maximum_fusion.1
  119.8 0.8 concatenate.244
  120.5 0.8 concatenate.228
  122.8 0.9 fusion.17
  123.7 1.1 fusion.41
  124.9 0.8 concatenate.255
  128.8 0.9 constant_dynamic-update-slice_fusion.28
  130.7 1.0 broadcast_in_dim.2
  131.7 1.4 copy.15
  133.1 1.6 fusion.10
  134.7 14.5 %all-reduce.3 = bf16[32,108]{1,0:T(8,128)(2,1)S(1)} all-reduce(bf16[32,108]{1,0:T(8,128)(2,1)S(1)} %fusion.10), channel_id=2, replica_groups=mesh['dp'=4,'sx'=4,'sy'=2] {'sx','sy'}, use_global_device_ids=true, to_apply=%region_1.2.clone | all-reduce | flops 3456 | bytes 13824
  149.2 19.0 %all-reduce.5 = (f32[4,108]{1,0:T(4,128)S(1)}, f32[8,864]{1,0:T(8,128)S(1)}) all-reduce(f32[4,108]{1,0:T(4,128)S(1)} %dynamic-slice_convert_fusion.1, f32[8,864]{1,0:T(8,128)S(1)} %dynamic-slice_convert_fusion), channel_id=1, replica_groups=mesh['dp'=4,'sx'=4,'sy'=2] {'dp'}, use_global_device_ids=true, to_apply=%region_2.3 | all-reduce | flops 7344 | bytes 58752 | tf_op jit(solution)/shard_map/psum | solution.py:107
  168.2 14.8 %all-gather = f32[8,4,108]{2,1,0:T(4,128)S(1)} all-gather(f32[1,4,108]{2,1,0:T(4,128)S(1)} %bitcast.186), channel_id=1, replica_groups=mesh['dp'=4,'sx'=4,'sy'=2] {'sx','sy'}, dimensions={0}, use_global_device_ids=true | all-gather | bytes 15552 | tf_op jit(solution)/shard_map/all_gather | solution.py:109
  183.0 16.1 %all_gather.7 = f32[64,864]{1,0:T(8,128)S(1)} all-gather(f32[8,864]{1,0:T(8,128)S(1)} %get-tuple-element.3), channel_id=1, replica_groups=mesh['dp'=4,'sx'=4,'sy'=2] {'sx','sy'}, dimensions={0}, use_global_device_ids=true | all-gather | bytes 248832 | tf_op jit(solution)/shard_map/all_gather | solution.py:110
  (122 shorter events, 13.2 us)
Async XLA Ops:
  7.2 20.8 %copy-start = (bf16[32,108]{1,0:T(8,128)(2,1)S(1)}, bf16[32,108]{1,0:T(8,128)(2,1)}, u32[]{:S(2)}) copy-start(bf16[32,108]{1,0:T(8,128)(2,1)} %param.5) | copy-start | bytes 20740
  7.2 19.3 %copy-start.1 = (bf16[1,4,4,8,128]{4,3,2,1,0:T(8,128)(2,1)S(1)}, bf16[1,4,4,8,128]{4,3,2,1,0:T(8,128)(2,1)}, u32[]{:S(2)}) copy-start(bf16[1,4,4,8,128]{4,3,2,1,0:T(8,128)(2,1)} %param.4) | copy-start | bytes 98308
  7.2 109.9 %all-reduce.8.cloned.1.call-start = ((), (), s32[]{:S(2)}) async-start(), calls=%async_computation | async-start | bytes 229376
  8.0 5.5 %collective-permute-start = (bf16[4,1,8,128]{3,2,1,0:T(8,128)(2,1)S(1)}, bf16[4,1,8,128]{3,2,1,0:T(8,128)(2,1)S(1)}, u32[]{:S(2)}, u32[]{:S(2)}) collective-permute-start(bf16[4,1,8,128]{3,2,1,0:T(8,128)(2,1)S(1)} %get-tuple-element.100), channel_id=1, source_target_pairs={{0,2},{2,4},{4,6},{1,3},{3,5},{5,7},{8,10},{10,12},{12,14},{9,11},... | collective-permute-start | bytes 24584 | tf_op jit(solution)/shard_map/ppermute | solution.py:12
  10.3 5.2 %collective-permute-start.1 = (bf16[4,1,8,128]{3,2,1,0:T(8,128)(2,1)S(1)}, bf16[4,1,8,128]{3,2,1,0:T(8,128)(2,1)S(1)}, u32[]{:S(2)}, u32[]{:S(2)}) collective-permute-start(bf16[4,1,8,128]{3,2,1,0:T(8,128)(2,1)S(1)} %get-tuple-element.101), channel_id=1, source_target_pairs={{2,0},{4,2},{6,4},{3,1},{5,3},{7,5},{10,8},{12,10},{14,12},{11,9},... | collective-permute-start | bytes 24584 | tf_op jit(solution)/shard_map/ppermute | solution.py:15
  16.4 5.6 %collective-permute-start.2 = (bf16[4,6,1,128]{3,2,1,0:T(2,128)(2,1)S(1)}, bf16[4,6,1,128]{3,2,1,0:T(2,128)(2,1)S(1)}, u32[]{:S(2)}, u32[]{:S(2)}) collective-permute-start(bf16[4,6,1,128]{3,2,1,0:T(2,128)(2,1)S(1)} %get-tuple-element.96), channel_id=1, source_target_pairs={{0,1},{2,3},{4,5},{6,7},{8,9},{10,11},{12,13},{14,15},{16,17},{18,... | collective-permute-start | bytes 18440 | tf_op jit(solution)/shard_map/ppermute | solution.py:12
  19.8 5.6 %collective-permute-start.3 = (bf16[4,6,1,128]{3,2,1,0:T(2,128)(2,1)S(1)}, bf16[4,6,1,128]{3,2,1,0:T(2,128)(2,1)S(1)}, u32[]{:S(2)}, u32[]{:S(2)}) collective-permute-start(bf16[4,6,1,128]{3,2,1,0:T(2,128)(2,1)S(1)} %get-tuple-element.97), channel_id=1, source_target_pairs={{1,0},{3,2},{5,4},{7,6},{9,8},{11,10},{13,12},{15,14},{17,16},{19,... | collective-permute-start | bytes 18440 | tf_op jit(solution)/shard_map/ppermute | solution.py:15
  31.0 5.6 %copy-start.10 = (u32[32]{0:T(128)S(1)}, u32[32]{0:T(128)}, u32[]{:S(2)}) copy-start(u32[32]{0:T(128)} %constant.33) | copy-start | bytes 388
  32.4 8.8 %collective-permute-start.4 = (bf16[32,1,4,64]{0,3,2,1:T(8,128)(2,1)S(1)}, bf16[32,1,4,64]{0,3,2,1:T(8,128)(2,1)S(1)}, u32[]{:S(2)}, u32[]{:S(2)}) collective-permute-start(bf16[32,1,4,64]{0,3,2,1:T(8,128)(2,1)S(1)} %get-tuple-element.86), channel_id=1, source_target_pairs={{0,2},{2,4},{4,6},{1,3},{3,5},{5,7},{8,10},{10,12},{12,14},{9,11},... | collective-permute-start | bytes 49160 | tf_op jit(solution)/shard_map/ppermute | solution.py:12
  35.3 5.9 %collective-permute-start.5 = (bf16[32,1,4,64]{0,3,2,1:T(8,128)(2,1)S(1)}, bf16[32,1,4,64]{0,3,2,1:T(8,128)(2,1)S(1)}, u32[]{:S(2)}, u32[]{:S(2)}) collective-permute-start(bf16[32,1,4,64]{0,3,2,1:T(8,128)(2,1)S(1)} %get-tuple-element.87), channel_id=1, source_target_pairs={{2,0},{4,2},{6,4},{3,1},{5,3},{7,5},{10,8},{12,10},{14,12},{11,9},... | collective-permute-start | bytes 49160 | tf_op jit(solution)/shard_map/ppermute | solution.py:15
  41.2 4.1 %collective-permute-start.6 = (bf16[32,4,1,64]{0,3,2,1:T(8,128)(2,1)S(1)}, bf16[32,4,1,64]{0,3,2,1:T(8,128)(2,1)S(1)}, u32[]{:S(2)}, u32[]{:S(2)}) collective-permute-start(bf16[32,4,1,64]{0,3,2,1:T(8,128)(2,1)S(1)} %get-tuple-element.59), channel_id=1, source_target_pairs={{0,1},{2,3},{4,5},{6,7},{8,9},{10,11},{12,13},{14,15},{16,17},{18,... | collective-permute-start | bytes 49160 | tf_op jit(solution)/shard_map/ppermute | solution.py:12
  43.2 6.2 %collective-permute-start.7 = (bf16[32,4,1,64]{0,3,2,1:T(8,128)(2,1)S(1)}, bf16[32,4,1,64]{0,3,2,1:T(8,128)(2,1)S(1)}, u32[]{:S(2)}, u32[]{:S(2)}) collective-permute-start(bf16[32,4,1,64]{0,3,2,1:T(8,128)(2,1)S(1)} %get-tuple-element.60), channel_id=1, source_target_pairs={{1,0},{3,2},{5,4},{7,6},{9,8},{11,10},{13,12},{15,14},{17,16},{19,... | collective-permute-start | bytes 49160 | tf_op jit(solution)/shard_map/ppermute | solution.py:15
  58.9 5.0 %collective-permute-start.8 = (bf16[64,1,4,64]{3,2,1,0:T(4,128)(2,1)S(1)}, bf16[64,1,4,64]{3,2,1,0:T(4,128)(2,1)S(1)}, u32[]{:S(2)}, u32[]{:S(2)}) collective-permute-start(bf16[64,1,4,64]{3,2,1,0:T(4,128)(2,1)S(1)} %get-tuple-element.83), channel_id=1, source_target_pairs={{0,2},{2,4},{4,6},{1,3},{3,5},{5,7},{8,10},{10,12},{12,14},{9,11},... | collective-permute-start | bytes 98312 | tf_op jit(solution)/shard_map/ppermute | solution.py:12
  62.6 5.8 %collective-permute-start.9 = (bf16[64,1,4,64]{3,2,1,0:T(4,128)(2,1)S(1)}, bf16[64,1,4,64]{3,2,1,0:T(4,128)(2,1)S(1)}, u32[]{:S(2)}, u32[]{:S(2)}) collective-permute-start(bf16[64,1,4,64]{3,2,1,0:T(4,128)(2,1)S(1)} %get-tuple-element.82), channel_id=1, source_target_pairs={{2,0},{4,2},{6,4},{3,1},{5,3},{7,5},{10,8},{12,10},{14,12},{11,9},... | collective-permute-start | bytes 98312 | tf_op jit(solution)/shard_map/ppermute | solution.py:15
  69.8 48.0 %collective-permute-start.10 = (bf16[64,4,1,64]{3,2,1,0:T(2,128)(2,1)S(1)}, bf16[64,4,1,64]{3,2,1,0:T(2,128)(2,1)S(1)}, u32[]{:S(2)}, u32[]{:S(2)}) collective-permute-start(bf16[64,4,1,64]{3,2,1,0:T(2,128)(2,1)S(1)} %get-tuple-element.55), channel_id=1, source_target_pairs={{0,1},{2,3},{4,5},{6,7},{8,9},{10,11},{12,13},{14,15},{16,17},{18,... | collective-permute-start | bytes 98312 | tf_op jit(solution)/shard_map/ppermute | solution.py:12
  71.4 46.4 %collective-permute-start.11 = (bf16[64,4,1,64]{3,2,1,0:T(2,128)(2,1)S(1)}, bf16[64,4,1,64]{3,2,1,0:T(2,128)(2,1)S(1)}, u32[]{:S(2)}, u32[]{:S(2)}) collective-permute-start(bf16[64,4,1,64]{3,2,1,0:T(2,128)(2,1)S(1)} %get-tuple-element.56), channel_id=1, source_target_pairs={{1,0},{3,2},{5,4},{7,6},{9,8},{11,10},{13,12},{15,14},{17,16},{19,... | collective-permute-start | bytes 98312 | tf_op jit(solution)/shard_map/ppermute | solution.py:15
  125.9 3.8 %copy-start.4 = (bf16[64,512]{1,0:T(8,128)(2,1)S(1)}, bf16[64,512]{1,0:T(8,128)(2,1)}, u32[]{:S(2)}) copy-start(bf16[64,512]{1,0:T(8,128)(2,1)} %concatenate.232) | copy-start | bytes 196612
  126.9 2.9 %copy-start.9 = (bf16[64,512]{1,0:T(8,128)(2,1)S(1)}, bf16[64,512]{1,0:T(8,128)(2,1)}, u32[]{:S(2)}) copy-start(bf16[64,512]{1,0:T(8,128)(2,1)} %concatenate.236) | copy-start | bytes 196612
  127.2 2.7 %copy-start.7 = (bf16[64,512]{1,0:T(8,128)(2,1)S(1)}, bf16[64,512]{1,0:T(8,128)(2,1)}, u32[]{:S(2)}) copy-start(bf16[64,512]{1,0:T(8,128)(2,1)} %concatenate.239) | copy-start | bytes 196612
  127.7 2.2 %copy-start.5 = (bf16[64,512]{1,0:T(8,128)(2,1)S(1)}, bf16[64,512]{1,0:T(8,128)(2,1)}, u32[]{:S(2)}) copy-start(bf16[64,512]{1,0:T(8,128)(2,1)} %concatenate.244) | copy-start | bytes 196612
  128.0 1.9 copy-start.3
  128.2 1.8 copy-start.8
  128.6 1.5 copy-start.6
  128.8 1.3 copy-start.2
Sparse Core Ops, SparseCore 0:
  62.7 54.2 all-reduce.7
where the time goes:
time: 209 us; the launch traced here: 207 us
  blocking collectives  64.4 us (31%)
  waiting for transfers between devices  58.3 us (28%)
  local copies, waits for them, and re-layouts  31.7 us (15%)
  starting transfers between devices  22.9 us (11%)
  between operations  16.2 us (8%)
  other arithmetic  8.13 us (4%)
  matrix products  5.72 us (3%)
    unnamed x2, waiting for transfers between devices  44.2 us
    psum x1, blocking collectives, shards(): shared = lax.psum((shared[0], shared[1]), 'dp')  19 us
    all_gather x1, blocking collectives, shards(): lax.all_gather(shared[1], ('sx', 'sy'), axis=0, tiled=True)  16.1 us
    concatenate x40, local copies, waits for them, and re-layouts, patches(): stacked = jnp.concatenate(columns, 0)  15.4 us
    ppermute x6, starting transfers between devices, padded_2(): lax.ppermute(lax.slice_in_dim(block, block.shape[dim] - width, None, axis...  15 us
    all_gather x1, blocking collectives, shards(): lax.all_gather(shared[0], ('sx', 'sy'), axis=0, tiled=True)  14.8 us
    unnamed x1, blocking collectives  14.5 us
    ppermute x6, waiting for transfers between devices, padded_2(): lax.ppermute(lax.slice_in_dim(block, 0, width, axis=dim), axis, backward)  14 us
  transfers between devices with their start and end apart: 13, of which 5 were waited for; matrix products, arithmetic and copies ran while one was open for 5% of the time, Pallas kernels for 0%

commit v1 on v0

v1 whole, which is shorter than its diff:
```python
import functools

import jax
import jax.numpy as jnp
from jax import lax
from jax.experimental import pallas as pl
from jax.experimental.pallas import tpu as pltpu
from jax.sharding import PartitionSpec as P

F32 = jnp.float32
BF16 = jnp.bfloat16
MESH = pl.DeviceIdType.MESH
DIRS = [(dx, dy) for dx in (-1, 0, 1) for dy in (-1, 0, 1) if (dx, dy) != (0, 0)]


def nt(a, b):
    return lax.dot_general(a, b, (((1,), (1,)), ((), ())), preferred_element_type=F32)


def nn(a, b):
    return jnp.dot(a, b, preferred_element_type=F32)


def iota(shape, dim):
    return lax.broadcasted_iota(jnp.int32, shape, dim)


def one_hot(cond):
    return jnp.where(cond, 1.0, 0.0).astype(BF16)


def slope(value):
    return 0.65 + 0.35 * jnp.tanh(0.5 * value)


def leaky(value):
    tail = jnp.log(1.0 + jnp.exp(-jnp.abs(value)))
    return 0.3 * value + 0.7 * (jnp.maximum(value, 0.0) + tail)


def kernel(
    nd, nx, ny,
    vol, w1, w2, cot,
    out1, out2,
    rows_f, vs, cot_f, cot_d, pool, q, bk, bs, slope1, w2t,
    g2s, g2r, g2d, ag, g1p, g1d,
    halo_send, halo_recv, plane_send, plane_recv, dp_send, dp_recv,
):
    dpi, ix, iy = lax.axis_index("dp"), lax.axis_index("sx"), lax.axis_index("sy")
    n_plane = nx * ny
    me = ix * ny + iy
    chans, X, Y, Z = vol.shape[1:]
    hx, hy, hz = X // 2, Y // 2, Z // 2
    inner, outer = w1.shape[0], w2.shape[0]
    rows = outer // n_plane
    taps = 3 * chans
    tap_rows = vs.shape[2]

    vs[...] = jnp.zeros_like(vs)
    pool[...] = jnp.zeros_like(pool)
    bk[...] = jnp.zeros_like(bk)

    def plane_id(r):
        peer = lax.rem(me + r, n_plane)
        return {"sx": peer // ny, "sy": lax.rem(peer, ny)}

    def dp_id(r):
        return {"dp": lax.rem(dpi + r, nd)}

    barrier = pltpu.get_barrier_semaphore()
    for r in range(1, n_plane):
        pl.semaphore_signal(barrier, inc=1, device_id=plane_id(r), device_id_type=MESH)
    for r in range(1, nd):
        pl.semaphore_signal(barrier, inc=1, device_id=dp_id(r), device_id_type=MESH)

    rows_f[...] = jnp.zeros_like(rows_f)
    lane = iota((Y, Z), 1)
    for c in range(chans):
        for x in range(X):
            v = vol[0, c, x].astype(F32)
            down = jnp.where(lane == 0, 0.0, pltpu.roll(v, 1, 1))
            up_z = jnp.where(lane == Z - 1, 0.0, pltpu.roll(v, Z - 1, 1))
            for e, moved in enumerate((down, v, up_z)):
                rows_f[pl.ds(x * Y * tap_rows + e * chans + c, Y, stride=tap_rows), :] = moved
    for x in range(X):
        for y in range(Y):
            start = (x * Y + y) * tap_rows
            vs[1 + x, 1 + y] = rows_f[start : start + tap_rows].astype(BF16)

    pl.semaphore_wait(barrier, n_plane - 1 + nd - 1)

    def there(dx, dy):
        ok = None
        for d, i, n in ((dx, ix, nx), (dy, iy, ny)):
            if d == 0:
                continue
            here = (i + d >= 0) & (i + d < n)
            ok = here if ok is None else ok & here
        return ok

    def side(d, n):
        if d == 0:
            return pl.ds(1, n), pl.ds(1, n)
        return (pl.ds(1, 1), pl.ds(n + 1, 1)) if d < 0 else (pl.ds(n, 1), pl.ds(0, 1))

    def halo(ref, stage):
        wide, high = ref.shape[0] - 2, ref.shape[1] - 2
        copies = []
        for i, (dx, dy) in enumerate(DIRS):
            (sx, tx), (sy, ty) = side(dx, wide), side(dy, high)
            copy = pltpu.make_async_remote_copy(
                src_ref=ref.at[sx, sy],
                dst_ref=ref.at[tx, ty],
                send_sem=halo_send.at[stage, i],
                recv_sem=halo_recv.at[stage, i],
                device_id={"sx": ix + dx, "sy": iy + dy},
                device_id_type=MESH,
            )
            pl.when(there(dx, dy))(copy.start)
            copies.append((copy, dx, dy))
        return copies

    def halo_arrived(copies):
        for copy, dx, dy in copies:
            pl.when(there(-dx, -dy))(copy.wait_recv)

    def halo_sent(copies):
        for copy, dx, dy in copies:
            pl.when(there(dx, dy))(copy.wait_send)

    def spread(count, ids, src, dst, send, recv, stage):
        copies = []
        for r in range(1, count):
            copy = pltpu.make_async_remote_copy(
                src_ref=src(r),
                dst_ref=dst,
                send_sem=send.at[stage, r],
                recv_sem=recv.at[stage, r],
                device_id=ids(r),
                device_id_type=MESH,
            )
            copy.start()
            copies.append(copy)
        return copies

    sent = []
    halos = [halo(vs, 0)]

    n12 = 9 * taps
    pick_r, pick_c = iota((n12, 9 * tap_rows), 0), iota((n12, 9 * tap_rows), 1)
    tap = lax.rem(pick_c, tap_rows)
    pick = one_hot((pick_r == (pick_c // tap_rows) * taps + tap) & (tap < taps))
    w1p = nn(w1[...], pick).astype(BF16)
    eye = one_hot(iota((128, 128), 0) == iota((128, 128), 1))
    width = w2.shape[1]
    for at in range(0, width, 128):
        n = min(128, width - at)
        w2t[at : at + n] = nt(eye[:n, :n], w2[:, at : at + n]).astype(BF16)
    for o in range(outer):
        for x in range(hx):
            start = (o * hx + x) * hy
            cot_f[start : start + hy] = cot[0, o, x].astype(F32)
    cells = hx * hy
    stack = jnp.concatenate(
        [cot_f[pl.ds(i, outer, stride=cells), :] for i in range(cells)], axis=0
    ).astype(BF16)
    double = one_hot(iota((hz, Z), 0) == iota((hz, Z), 1) // 2)
    doubled = nn(stack, double)
    for i in range(cells):
        cot_d[:, i * Z : (i + 1) * Z] = doubled[i * outer : (i + 1) * outer]
    pool_m = one_hot(lax.rem(iota((4 * Z, Z), 0), Z) // 2 == iota((4 * Z, Z), 1) // 2)
    t_in, t_out = iota((Z, 2 * Z), 0), iota((Z, 2 * Z), 1)
    shift_m = one_hot(t_in == jnp.where(t_out < Z, t_out - 2, t_out - Z + 2))

    halo_arrived(halos[0])

    def fine_cols(x):
        return jnp.concatenate(
            [
                jnp.concatenate([vs[x + a, y + b] for y in range(Y)], axis=1)
                for a in range(3)
                for b in range(3)
            ],
            axis=0,
        )

    for xc in range(hx):
        hid = []
        for x in (2 * xc, 2 * xc + 1):
            pre = nn(w1p, fine_cols(x))
            slope1[x] = pre
            hid.append(leaky(pre).astype(BF16))
        block = jnp.concatenate(
            [
                jnp.concatenate(
                    [
                        hid[i][:, (2 * yc + j) * Z : (2 * yc + j + 1) * Z]
                        for i in range(2)
                        for j in range(2)
                    ],
                    axis=1,
                )
                for yc in range(hy)
            ],
            axis=0,
        )
        mean = (nn(block, pool_m) * 0.125).astype(BF16)
        for yc in range(hy):
            pool[1 + xc, 1 + yc] = mean[yc * inner : (yc + 1) * inner]
    halos.append(halo(pool, 1))

    inside = [(x, y) for x in range(1, hx + 1) for y in range(1, hy + 1)]
    rim = [
        (x, y) for x in range(hx + 2) for y in range(hy + 2) if (x, y) not in inside
    ]

    def shifts(src, dst, places, order):
        n = src.shape[2]
        tiles = jnp.concatenate([src[x, y] for x, y in places], axis=0)
        moved = nn(tiles, shift_m).astype(BF16)
        for i, (x, y) in enumerate(places):
            part = moved[i * n : (i + 1) * n]
            dst[x, y, order[0] * n : (order[0] + 1) * n] = part[:, :Z]
            dst[x, y, n : 2 * n] = tiles[i * n : (i + 1) * n]
            dst[x, y, order[1] * n : (order[1] + 1) * n] = part[:, Z:]

    for x in range(X):
        slope1[x] = slope(slope1[x]) * 0.125
    shifts(pool, q, inside, (0, 2))
    halo_arrived(halos[1])
    shifts(pool, q, rim, (0, 2))

    places = [(x, y) for x in range(hx) for y in range(hy)]

    def coarse_cols():
        return jnp.concatenate(
            [
                jnp.concatenate([q[x + a, y + b] for x, y in places], axis=1)
                for a in range(3)
                for b in range(3)
            ],
            axis=0,
        )

    pre_second = nn(w2[...], coarse_cols())
    back = (cot_d[...] * slope(pre_second)).astype(BF16)
    for i, (x, y) in enumerate(places):
        bk[1 + x, 1 + y] = back[:, i * Z : (i + 1) * Z]
    halos.append(halo(bk, 2))

    count = cells * hz * nd * n_plane
    scale_second, scale_first = count**-0.5, (8 * count) ** -0.5
    grad2 = nt(back, coarse_cols()) * (0.5 * scale_second)
    for i in range(n_plane):
        g2s[i] = grad2[i * rows : (i + 1) * rows].astype(BF16)
    g2r[me] = g2s[me]
    in_plane = lambda r: g2s.at[lax.rem(me + r, n_plane)]
    scatter = spread(n_plane, plane_id, in_plane, g2r.at[me], plane_send, plane_recv, 0)
    sent += scatter

    shifts(bk, bs, inside, (2, 0))
    halo_arrived(halos[2])
    shifts(bk, bs, rim, (2, 0))
    total = jnp.zeros((inner, cells * Z), F32)
    for a in range(3):
        for b in range(3):
            for e in range(3):
                k = (a * 3 + b) * 3 + e
                rhs = jnp.concatenate(
                    [
                        bs[x + 2 - a, y + 2 - b, e * outer : (e + 1) * outer]
                        for x, y in places
                    ],
                    axis=1,
                )
                total = total + nn(w2t[k * inner : (k + 1) * inner], rhs)

    for copy in scatter:
        copy.wait_recv()
    acc = jnp.zeros((rows, width), F32)
    for i in range(n_plane):
        acc = acc + g2r[i].astype(F32)
    g2d[dpi] = acc.astype(BF16)
    own = lambda ref, i: (lambda r: ref.at[i])
    across = spread(nd, dp_id, own(g2d, dpi), g2d.at[dpi], dp_send, dp_recv, 0)
    sent += across

    grad1 = jnp.zeros((inner, 9 * tap_rows), F32)
    for x in range(X):
        lower = []
        for y in range(Y):
            at = ((x // 2) * hy + y // 2) * Z
            lower.append(total[:, at : at + Z] * slope1[x, :, y * Z : (y + 1) * Z])
        low = jnp.concatenate(lower, axis=1).astype(BF16)
        grad1 = grad1 + nt(low, fine_cols(x))
    grad1 = nt((grad1 * scale_first).astype(BF16), pick)
    g1p[me] = grad1.astype(BF16)
    firsts = spread(n_plane, plane_id, own(g1p, me), g1p.at[me], plane_send, plane_recv, 1)
    sent += firsts

    for copy in across:
        copy.wait_recv()
    acc = jnp.zeros((rows, width), F32)
    for i in range(nd):
        acc = acc + g2d[i].astype(F32)
    ag[me] = acc.astype(BF16)
    gather = spread(n_plane, plane_id, own(ag, me), ag.at[me], plane_send, plane_recv, 2)
    sent += gather

    for copy in firsts:
        copy.wait_recv()
    acc = jnp.zeros(out1.shape, F32)
    for i in range(n_plane):
        acc = acc + g1p[i].astype(F32)
    g1d[dpi] = acc.astype(BF16)
    last = spread(nd, dp_id, own(g1d, dpi), g1d.at[dpi], dp_send, dp_recv, 1)
    sent += last

    for copy in gather:
        copy.wait_recv()
    for i in range(n_plane):
        out2[i * rows : (i + 1) * rows] = ag[i].astype(F32)
    for copy in last:
        copy.wait_recv()
    acc = jnp.zeros(out1.shape, F32)
    for i in range(nd):
        acc = acc + g1d[i].astype(F32)
    out1[...] = acc
    for copies in halos:
        halo_sent(copies)
    for copy in sent:
        copy.wait_send()


def shards(nd, nx, ny, volume, first_weight, second_weight, cotangent):
    _, chans, X, Y, Z = volume.shape
    inner, outer = first_weight.shape[0], second_weight.shape[0]
    width = second_weight.shape[1]
    hx, hy, hz = X // 2, Y // 2, Z // 2
    cells = hx * hy
    n_plane = nx * ny
    rows = outer // n_plane
    tap_rows = -(-3 * chans // 16) * 16
    vmem = pl.BlockSpec(memory_space=pltpu.VMEM)
    dma = pltpu.SemaphoreType.DMA
    return pl.pallas_call(
        functools.partial(kernel, nd, nx, ny),
        out_shape=(
            jax.ShapeDtypeStruct(first_weight.shape, F32),
            jax.ShapeDtypeStruct(second_weight.shape, F32),
        ),
        in_specs=[vmem] * 4,
        out_specs=(vmem, vmem),
        scratch_shapes=[
            pltpu.VMEM((X * Y * tap_rows, Z), F32),
            pltpu.VMEM((X + 2, Y + 2, tap_rows, Z), BF16),
            pltpu.VMEM((outer * cells, hz), F32),
            pltpu.VMEM((outer, cells * Z), F32),
            pltpu.VMEM((hx + 2, hy + 2, inner, Z), BF16),
            pltpu.VMEM((hx + 2, hy + 2, 3 * inner, Z), BF16),
            pltpu.VMEM((hx + 2, hy + 2, outer, Z), BF16),
            pltpu.VMEM((hx + 2, hy + 2, 3 * outer, Z), BF16),
            pltpu.VMEM((X, inner, Y * Z), F32),
            pltpu.VMEM((width, outer), BF16),
            pltpu.VMEM((n_plane, rows, width), BF16),
            pltpu.VMEM((n_plane, rows, width), BF16),
            pltpu.VMEM((nd, rows, width), BF16),
            pltpu.VMEM((n_plane, rows, width), BF16),
            pltpu.VMEM((n_plane,) + first_weight.shape, BF16),
            pltpu.VMEM((nd,) + first_weight.shape, BF16),
            dma((3, 8)),
            dma((3, 8)),
            dma((3, n_plane)),
            dma((3, n_plane)),
            dma((2, nd)),
            dma((2, nd)),
        ],
        compiler_params=pltpu.CompilerParams(
            collective_id=0, has_side_effects=True, vmem_limit_bytes=48 * 1024 * 1024
        ),
        name="step",
    )(volume, first_weight, second_weight, cotangent)


def solution(mesh):
    sizes = dict(mesh.shape)
    return jax.shard_map(
        functools.partial(shards, sizes["dp"], sizes["sx"], sizes["sy"]),
        mesh=mesh,
        in_specs=(P("dp", None, "sx", "sy", None), P(), P(), P("dp", None, "sx", "sy", None)),
        out_specs=(P(), P()),
        check_vma=False,
    )
```

time: 209 us -> 32.1 us (0.15)
  blocking collectives: 64.4 us -> 0 us
  waiting for transfers between devices: 58.3 us -> 0 us
  local copies, waits for them, and re-layouts: 31.7 us -> 4.54 us
  Pallas kernels: 0 us -> 26.6 us
  starting transfers between devices: 22.9 us -> 0 us
  between operations: 16.2 us -> 0.65 us
  other arithmetic: 8.13 us -> 0 us
  matrix products: 5.72 us -> 0 us
    unnamed x2 -> x0, waiting for transfers between devices: 44.2 us -> none
    all_gather x2 -> x0, blocking collectives: 30.9 us -> none  [the longest x1 16.1 us: shards(): lax.all_gather(shared[1], ('sx', 'sy'), axis=0, tiled=True)]
    pallas_call x0 -> x1, Pallas kernels: none -> 26.6 us  [shards(): pl.pallas_call(functools.partial(kernel, nd, nx, ny), out_shape=(jax.Shap...]
    ppermute x12 -> x0, starting transfers between devices: 22.9 us -> none  [the longest x6 15 us: padded_2(): lax.ppermute(lax.slice_in_dim(block, block.shape[dim] - width, None, axis...]
    psum x1 -> x0, blocking collectives: 19 us -> none  [shards(): shared = lax.psum((shared[0], shared[1]), 'dp')]
    concatenate x41 -> x0, local copies, waits for them, and re-layouts: 15.4 us -> none  [the longest x40 15.4 us: patches(): stacked = jnp.concatenate(columns, 0)]
    unnamed x1 -> x0, blocking collectives: 14.5 us -> none
    ppermute x12 -> x0, waiting for transfers between devices: 14 us -> none  [the longest x6 14 us: padded_2(): lax.ppermute(lax.slice_in_dim(block, 0, width, axis=dim), axis, backward)]
  transfers between devices with their start and end apart: 13 -> 0, of which waited for: 5 -> 0; matrix products, arithmetic and copies ran while one was open for 5% -> 0% of each run, Pallas kernels for 0% -> 0%
where the time goes in v1:
time: 32.1 us; the launch traced here: 31.8 us
  Pallas kernels  26.6 us (83%)
  local copies, waits for them, and re-layouts  4.54 us (14%)
  between operations  0.65 us (2%)
    pallas_call x1, Pallas kernels, shards(): pl.pallas_call(functools.partial(kernel, nd, nx, ny), out_shape=(jax.Shap...  26.6 us
    unnamed x10, local copies, waits for them, and re-layouts  4.54 us

profile of v1, /device:TPU:0, one launch (start us, length us, event | category | flops | bytes accessed | tf_op | source)
XLA Modules:
  0.0 31.8 jit_solution(14528955386758314097)
XLA Ops:
  0.6 0.0 copy-start
  0.6 0.9 %copy-done = bf16[1,64,2,4,64]{4,3,2,1,0:T(4,128)(2,1)S(1)} copy-done((bf16[1,64,2,4,64]{4,3,2,1,0:T(4,128)(2,1)S(1)}, bf16[1,64,2,4,64]{4,3,2,1,0:T(4,128)(2,1)}, u32[]{:S(2)}) %copy-start) | copy-done | bytes 65560
  1.5 0.0 copy-start.1
  1.5 0.9 %copy-done.1 = bf16[64,864]{1,0:T(8,128)(2,1)S(1)} copy-done((bf16[64,864]{1,0:T(8,128)(2,1)S(1)}, bf16[64,864]{1,0:T(8,128)(2,1)}, u32[]{:S(2)}) %copy-start.1) | copy-done | bytes 110616
  2.4 0.0 copy-start.2
  2.4 0.8 %copy-done.2 = bf16[1,4,4,8,128]{4,3,2,1,0:T(8,128)(2,1)S(1)} copy-done((bf16[1,4,4,8,128]{4,3,2,1,0:T(8,128)(2,1)S(1)}, bf16[1,4,4,8,128]{4,3,2,1,0:T(8,128)(2,1)}, u32[]{:S(2)}) %copy-start.2) | copy-done | bytes 32792
  3.2 0.0 copy-start.3
  3.2 0.7 %copy-done.3 = bf16[32,108]{1,0:T(8,128)(2,1)S(1)} copy-done((bf16[32,108]{1,0:T(8,128)(2,1)S(1)}, bf16[32,108]{1,0:T(8,128)(2,1)}, u32[]{:S(2)}) %copy-start.3) | copy-done | bytes 6936
  3.9 26.6 %step.1 = (f32[32,108]{1,0:T(8,128)S(1)}, f32[64,864]{1,0:T(8,128)S(1)}) custom-call(bf16[1,4,4,8,128]{4,3,2,1,0:T(8,128)(2,1)S(1)} %copy-done.2, bf16[32,108]{1,0:T(8,128)(2,1)S(1)} %copy-done.3, bf16[64,864]{1,0:T(8,128)(2,1)S(1)} %copy-done.1, bf16[1,64,2,4,64]{4,3,2,1,0:T(4,128)(2,1)S(1)} %copy-done), custom_call_target="tpu_custom_call" | custom-call | tf_op jit(solution)/shard_map/step/pallas_call | solution.py:346
  30.5 0.6 %copy.8 = f32[32,108]{1,0:T(8,128)} copy(f32[32,108]{1,0:T(8,128)S(1)} %get-tuple-element.4) | data formatting | bytes 27648
  31.1 0.7 %copy.9 = f32[64,864]{1,0:T(8,128)} copy(f32[64,864]{1,0:T(8,128)S(1)} %get-tuple-element.5) | data formatting | bytes 442368
Async XLA Ops:
  0.6 0.9 %copy-start = (bf16[1,64,2,4,64]{4,3,2,1,0:T(4,128)(2,1)S(1)}, bf16[1,64,2,4,64]{4,3,2,1,0:T(4,128)(2,1)}, u32[]{:S(2)}) copy-start(bf16[1,64,2,4,64]{4,3,2,1,0:T(4,128)(2,1)} %cot.1) | copy-start | bytes 196612
  1.5 0.9 %copy-start.1 = (bf16[64,864]{1,0:T(8,128)(2,1)S(1)}, bf16[64,864]{1,0:T(8,128)(2,1)}, u32[]{:S(2)}) copy-start(bf16[64,864]{1,0:T(8,128)(2,1)} %w2.1) | copy-start | bytes 331780
  2.4 0.8 %copy-start.2 = (bf16[1,4,4,8,128]{4,3,2,1,0:T(8,128)(2,1)S(1)}, bf16[1,4,4,8,128]{4,3,2,1,0:T(8,128)(2,1)}, u32[]{:S(2)}) copy-start(bf16[1,4,4,8,128]{4,3,2,1,0:T(8,128)(2,1)} %vol.1) | copy-start | bytes 98308
  3.2 0.7 %copy-start.3 = (bf16[32,108]{1,0:T(8,128)(2,1)S(1)}, bf16[32,108]{1,0:T(8,128)(2,1)}, u32[]{:S(2)}) copy-start(bf16[32,108]{1,0:T(8,128)(2,1)} %w1.1) | copy-start | bytes 20740

commit v2 on v1

v2 whole, which is shorter than its diff:
```python
import functools

import jax
import jax.numpy as jnp
from jax import lax
from jax.experimental import pallas as pl
from jax.experimental.pallas import tpu as pltpu
from jax.sharding import PartitionSpec as P

F32 = jnp.float32
BF16 = jnp.bfloat16
MESH = pl.DeviceIdType.MESH
REACH = 3
DIRS = [(dx, dy) for dx in (-1, 0, 1) for dy in (-1, 0, 1) if (dx, dy) != (0, 0)]


def nt(a, b):
    return lax.dot_general(a, b, (((1,), (1,)), ((), ())), preferred_element_type=F32)


def nn(a, b):
    return jnp.dot(a, b, preferred_element_type=F32)


def iota(shape, dim):
    return lax.broadcasted_iota(jnp.int32, shape, dim)


def one_hot(cond):
    return jnp.where(cond, 1.0, 0.0).astype(BF16)


def slope(value):
    return 0.65 + 0.35 * jnp.tanh(0.5 * value)


def leaky(value):
    tail = jnp.log(1.0 + jnp.exp(-jnp.abs(value)))
    return 0.3 * value + 0.7 * (jnp.maximum(value, 0.0) + tail)


def kernel(
    nd, nx, ny,
    vol_h, w1_h, w2_h, cot_h,
    out1, out2,
    vol, w1, w2, cot,
    raw, rows_f, vs, cot_f, cot_d, q, ups, slope1, w2t,
    g2s, g2r, g2d, ag, g1p, g1d,
    halo_send, halo_recv, plane_send, plane_recv, dp_send, dp_recv, fetch_sem,
):
    fetches = [
        pltpu.make_async_copy(src, dst, fetch_sem.at[i])
        for i, (src, dst) in enumerate(((vol_h, vol), (w1_h, w1), (w2_h, w2), (cot_h, cot)))
    ]
    for fetch in fetches:
        fetch.start()
    dpi, ix, iy = lax.axis_index("dp"), lax.axis_index("sx"), lax.axis_index("sy")
    n_plane = nx * ny
    me = ix * ny + iy
    chans, X, Y, Z = vol.shape[1:]
    hx, hy, hz = X // 2, Y // 2, Z // 2
    inner, outer = w1.shape[0], w2.shape[0]
    rows = outer // n_plane
    taps = 3 * chans
    tap_rows = vs.shape[2]

    raw[...] = jnp.zeros_like(raw)

    def plane_id(r):
        peer = lax.rem(me + r, n_plane)
        return {"sx": peer // ny, "sy": lax.rem(peer, ny)}

    def dp_id(r):
        return {"dp": lax.rem(dpi + r, nd)}

    barrier = pltpu.get_barrier_semaphore()
    for r in range(1, n_plane):
        pl.semaphore_signal(barrier, inc=1, device_id=plane_id(r), device_id_type=MESH)
    for r in range(1, nd):
        pl.semaphore_signal(barrier, inc=1, device_id=dp_id(r), device_id_type=MESH)

    def inside(d, i, n):
        return (i + d >= 0) & (i + d < n)

    def there(dx, dy):
        if dx == 0:
            return inside(dy, iy, ny)
        if dy == 0:
            return inside(dx, ix, nx)
        return inside(dx, ix, nx) & inside(dy, iy, ny)

    def xs(dx):
        return {-1: range(X - REACH, X), 0: range(X), 1: range(REACH)}[dx]

    halos = []
    for i, (dx, dy) in enumerate(DIRS):
        span = xs(-dx)
        part = pl.ds(span[0], len(span))
        copy = pltpu.make_async_remote_copy(
            src_ref=vol.at[0, :, part],
            dst_ref=raw.at[DIRS.index((-dx, -dy)), :, part],
            send_sem=halo_send.at[i],
            recv_sem=halo_recv.at[i],
            device_id={"sx": ix + dx, "sy": iy + dy},
            device_id_type=MESH,
        )
        halos.append((copy, dx, dy))

    rows_f[...] = jnp.zeros_like(rows_f)
    fetches[0].wait()
    pl.semaphore_wait(barrier, n_plane - 1 + nd - 1)
    for copy, dx, dy in halos:
        pl.when(there(dx, dy))(copy.start)

    def spread(count, ids, src, dst, send, recv, stage):
        copies = []
        for r in range(1, count):
            copy = pltpu.make_async_remote_copy(
                src_ref=src(r),
                dst_ref=dst,
                send_sem=send.at[stage, r],
                recv_sem=recv.at[stage, r],
                device_id=ids(r),
                device_id_type=MESH,
            )
            copy.start()
            copies.append(copy)
        return copies

    lane = iota((Y, Z), 1)

    def lay(src, dx, dy):
        for c in range(chans):
            for x in xs(dx):
                v = src(c, x).astype(F32)
                down = jnp.where(lane == 0, 0.0, pltpu.roll(v, 1, 1))
                up_z = jnp.where(lane == Z - 1, 0.0, pltpu.roll(v, Z - 1, 1))
                first = ((x + dx * X + REACH) * 3 + dy + 1) * Y
                for e, moved in enumerate((down, v, up_z)):
                    at = first * tap_rows + e * chans + c
                    rows_f[pl.ds(at, Y, stride=tap_rows), :] = moved

    def pack(x, y):
        start = (x * 3 * Y + y + Y - REACH) * tap_rows
        vs[x, y] = rows_f[start : start + tap_rows].astype(BF16)

    lay(lambda c, x: vol[0, c, x], 0, 0)
    own = [(x, y) for x in range(REACH, X + REACH) for y in range(REACH, Y + REACH)]
    for x, y in own:
        pack(x, y)
    for fetch in fetches[1:]:
        fetch.wait()
    n12 = 9 * taps
    pick_r, pick_c = iota((n12, 9 * tap_rows), 0), iota((n12, 9 * tap_rows), 1)
    tap = lax.rem(pick_c, tap_rows)
    pick = one_hot((pick_r == (pick_c // tap_rows) * taps + tap) & (tap < taps))
    w1p = nn(w1[...], pick).astype(BF16)
    eye = one_hot(iota((128, 128), 0) == iota((128, 128), 1))
    width = w2.shape[1]
    for at in range(0, width, 128):
        n = min(128, width - at)
        w2t[at : at + n] = nt(eye[:n, :n], w2[:, at : at + n]).astype(BF16)
    for o in range(outer):
        for x in range(hx):
            start = (o * hx + x) * hy
            cot_f[start : start + hy] = cot[0, o, x].astype(F32)
    cells = hx * hy
    stack = jnp.concatenate(
        [cot_f[pl.ds(i, outer, stride=cells), :] for i in range(cells)], axis=0
    ).astype(BF16)
    double = one_hot(iota((hz, Z), 0) == iota((hz, Z), 1) // 2)
    doubled = nn(stack, double)
    for i in range(cells):
        cot_d[:, i * Z : (i + 1) * Z] = doubled[i * outer : (i + 1) * outer]
    p_in, p_out = iota((4 * Z, 3 * Z), 0), iota((4 * Z, 3 * Z), 1)
    pool_m = one_hot(
        lax.rem(p_in, Z) // 2 == lax.rem(p_out, Z) // 2 + p_out // Z - 1
    )
    t_in, t_out = iota((Z, 2 * Z), 0), iota((Z, 2 * Z), 1)
    shift_m = one_hot(t_in == jnp.where(t_out < Z, t_out + 2, t_out - Z - 2))

    def present(d, i, n):
        return jnp.where(inside(d, i, n), 1.0, 0.0) if d else 1.0

    in_x = {d: present(d, ix, nx) for d in (-1, 0, 1)}
    in_y = {d: present(d, iy, ny) for d in (-1, 0, 1)}

    def part_of(at, rim, size):
        return -1 if at < rim else (1 if at >= rim + size else 0)

    def masked(value, at_x, at_y):
        if at_x:
            value = value * in_x[at_x]
        if at_y:
            value = value * in_y[at_y]
        return value

    for copy, dx, dy in halos:
        pl.when(there(-dx, -dy))(copy.wait_recv)
    for i, (dx, dy) in enumerate(DIRS):
        lay(lambda c, x, i=i: raw[i, c, x], dx, dy)
    for x in range(X + 2 * REACH):
        for y in range(Y + 2 * REACH):
            if (x, y) not in own:
                pack(x, y)

    wide, high = X + 4, Y + 4

    def fine_cols(x):
        return jnp.concatenate(
            [
                jnp.concatenate([vs[x + a, y + b] for y in range(high)], axis=1)
                for a in range(3)
                for b in range(3)
            ],
            axis=0,
        )

    for xc in range(hx + 2):
        hid = []
        for x in (2 * xc, 2 * xc + 1):
            pre = nn(w1p, fine_cols(x))
            slope1[x] = pre
            hid.append(leaky(pre).astype(BF16))
        block = jnp.concatenate(
            [
                jnp.concatenate(
                    [
                        hid[i][:, (2 * yc + j) * Z : (2 * yc + j + 1) * Z]
                        for i in range(2)
                        for j in range(2)
                    ],
                    axis=1,
                )
                for yc in range(hy + 2)
            ],
            axis=0,
        )
        mean = nn(block, pool_m) * 0.125
        for yc in range(hy + 2):
            tile = mean[yc * inner : (yc + 1) * inner]
            tile = masked(tile, part_of(xc, 1, hx), part_of(yc, 1, hy)).astype(BF16)
            for e in range(3):
                q[xc, yc, e * inner : (e + 1) * inner] = tile[:, e * Z : (e + 1) * Z]

    places = [(x, y) for x in range(hx) for y in range(hy)]

    def coarse_cols():
        return jnp.concatenate(
            [
                jnp.concatenate([q[x + a, y + b] for x, y in places], axis=1)
                for a in range(3)
                for b in range(3)
            ],
            axis=0,
        )

    pre_second = nn(w2[...], coarse_cols())
    back = (cot_d[...] * slope(pre_second)).astype(BF16)

    count = cells * hz * nd * n_plane
    scale_second, scale_first = count**-0.5, (8 * count) ** -0.5
    grad2 = nt(back, coarse_cols()) * (0.5 * scale_second)
    for i in range(n_plane):
        g2s[i] = grad2[i * rows : (i + 1) * rows].astype(BF16)
    g2r[me] = g2s[me]
    in_plane = lambda r: g2s.at[lax.rem(me + r, n_plane)]
    scatter = spread(n_plane, plane_id, in_plane, g2r.at[me], plane_send, plane_recv, 0)
    sent = list(scatter)

    tiles = jnp.concatenate([back[:, i * Z : (i + 1) * Z] for i in range(cells)], axis=0)
    moved = nn(tiles, shift_m).astype(BF16)

    def flat(value, half):
        return jnp.concatenate(
            [
                value[i * outer : (i + 1) * outer, half * Z : (half + 1) * Z]
                for i in range(cells)
            ],
            axis=1,
        )

    share = None
    for e, rhs in enumerate((flat(moved, 0), back, flat(moved, 1))):
        lhs = jnp.concatenate(
            [w2t[(3 * ab + e) * inner : (3 * ab + e + 1) * inner] for ab in range(9)],
            axis=0,
        )
        term = nn(lhs, rhs)
        share = term if share is None else share + term
    for xe in range(hx + 2):
        for ye in range(hy + 2):
            total = None
            for a in range(3):
                for b in range(3):
                    x, y = xe - a, ye - b
                    if 0 <= x < hx and 0 <= y < hy:
                        ab, at = 3 * a + b, (x * hy + y) * Z
                        term = share[ab * inner : (ab + 1) * inner, at : at + Z]
                        total = term if total is None else total + term
            ups[xe, ye] = masked(total * 0.125, part_of(xe, 1, hx), part_of(ye, 1, hy))

    for x in range(wide):
        slope1[x] = slope(slope1[x])

    for copy in scatter:
        copy.wait_recv()
    acc = jnp.zeros((rows, width), F32)
    for i in range(n_plane):
        acc = acc + g2r[i].astype(F32)
    g2d[dpi] = acc.astype(BF16)
    held = lambda ref, i: (lambda r: ref.at[i])
    across = spread(nd, dp_id, held(g2d, dpi), g2d.at[dpi], dp_send, dp_recv, 0)
    sent += across

    grad1 = jnp.zeros((inner, 9 * tap_rows), F32)
    for x in range(wide):
        low = jnp.concatenate(
            [ups[x // 2, y // 2] * slope1[x, :, y * Z : (y + 1) * Z] for y in range(high)],
            axis=1,
        ).astype(BF16)
        grad1 = grad1 + nt(low, fine_cols(x))
    grad1 = nt((grad1 * scale_first).astype(BF16), pick)
    g1p[me] = grad1.astype(BF16)
    firsts = spread(n_plane, plane_id, held(g1p, me), g1p.at[me], plane_send, plane_recv, 1)
    sent += firsts

    for copy in across:
        copy.wait_recv()
    acc = jnp.zeros((rows, width), F32)
    for i in range(nd):
        acc = acc + g2d[i].astype(F32)
    ag[me] = acc.astype(BF16)
    gather = spread(n_plane, plane_id, held(ag, me), ag.at[me], plane_send, plane_recv, 2)
    sent += gather

    for copy in firsts:
        copy.wait_recv()
    acc = jnp.zeros(out1.shape, F32)
    for i in range(n_plane):
        acc = acc + g1p[i].astype(F32)
    g1d[dpi] = acc.astype(BF16)
    last = spread(nd, dp_id, held(g1d, dpi), g1d.at[dpi], dp_send, dp_recv, 1)
    sent += last

    for copy in gather:
        copy.wait_recv()
    for i in range(n_plane):
        out2[i * rows : (i + 1) * rows] = ag[i].astype(F32)
    for copy in last:
        copy.wait_recv()
    acc = jnp.zeros(out1.shape, F32)
    for i in range(nd):
        acc = acc + g1d[i].astype(F32)
    out1[...] = acc
    for copy, dx, dy in halos:
        pl.when(there(dx, dy))(copy.wait_send)
    for copy in sent:
        copy.wait_send()


def shards(nd, nx, ny, volume, first_weight, second_weight, cotangent):
    _, chans, X, Y, Z = volume.shape
    inner, outer = first_weight.shape[0], second_weight.shape[0]
    width = second_weight.shape[1]
    hx, hy, hz = X // 2, Y // 2, Z // 2
    cells = hx * hy
    n_plane = nx * ny
    rows = outer // n_plane
    tap_rows = -(-3 * chans // 16) * 16
    vmem = pl.BlockSpec(memory_space=pltpu.VMEM)
    dma = pltpu.SemaphoreType.DMA
    return pl.pallas_call(
        functools.partial(kernel, nd, nx, ny),
        out_shape=(
            jax.ShapeDtypeStruct(first_weight.shape, F32),
            jax.ShapeDtypeStruct(second_weight.shape, F32),
        ),
        in_specs=[pl.BlockSpec(memory_space=pltpu.HBM)] * 4,
        out_specs=(vmem, vmem),
        scratch_shapes=[
            pltpu.VMEM(volume.shape, BF16),
            pltpu.VMEM(first_weight.shape, BF16),
            pltpu.VMEM(second_weight.shape, BF16),
            pltpu.VMEM(cotangent.shape, BF16),
            pltpu.VMEM((8,) + volume.shape[1:], BF16),
            pltpu.VMEM(((X + 2 * REACH) * 3 * Y * tap_rows, Z), F32),
            pltpu.VMEM((X + 2 * REACH, Y + 2 * REACH, tap_rows, Z), BF16),
            pltpu.VMEM((outer * cells, hz), F32),
            pltpu.VMEM((outer, cells * Z), F32),
            pltpu.VMEM((hx + 2, hy + 2, 3 * inner, Z), BF16),
            pltpu.VMEM((hx + 2, hy + 2, inner, Z), F32),
            pltpu.VMEM((X + 4, inner, (Y + 4) * Z), F32),
            pltpu.VMEM((width, outer), BF16),
            pltpu.VMEM((n_plane, rows, width), BF16),
            pltpu.VMEM((n_plane, rows, width), BF16),
            pltpu.VMEM((nd, rows, width), BF16),
            pltpu.VMEM((n_plane, rows, width), BF16),
            pltpu.VMEM((n_plane,) + first_weight.shape, BF16),
            pltpu.VMEM((nd,) + first_weight.shape, BF16),
            dma((8,)),
            dma((8,)),
            dma((3, n_plane)),
            dma((3, n_plane)),
            dma((2, nd)),
            dma((2, nd)),
            dma((4,)),
        ],
        compiler_params=pltpu.CompilerParams(
            collective_id=0, has_side_effects=True, vmem_limit_bytes=60 * 1024 * 1024
        ),
        name="step",
    )(volume, first_weight, second_weight, cotangent)


def solution(mesh):
    sizes = dict(mesh.shape)
    return jax.shard_map(
        functools.partial(shards, sizes["dp"], sizes["sx"], sizes["sy"]),
        mesh=mesh,
        in_specs=(P("dp", None, "sx", "sy", None), P(), P(), P("dp", None, "sx", "sy", None)),
        out_specs=(P(), P()),
        check_vma=False,
    )
```

time: 32.1 us -> 29.5 us (0.919)
  local copies, waits for them, and re-layouts: 4.54 us -> 2.96 us
  Pallas kernels: 26.6 us -> 25.7 us
    unnamed x10 -> x2, local copies, waits for them, and re-layouts: 4.54 us -> 2.96 us
    pallas_call x1, Pallas kernels: 26.6 us -> 25.7 us  [shards(): pl.pallas_call(functools.partial(kernel, nd, nx, ny), out_shape=(jax.Shap...]
where the time goes in v2:
time: 29.5 us; the launch traced here: 29.3 us
  Pallas kernels  25.7 us (87%)
  local copies, waits for them, and re-layouts  2.96 us (10%)
  between operations  0.64 us (2%)
    pallas_call x1, Pallas kernels, shards(): pl.pallas_call(functools.partial(kernel, nd, nx, ny), out_shape=(jax.Shap...  25.7 us
    unnamed x2, local copies, waits for them, and re-layouts  2.96 us

profile of v2, /device:TPU:0, one launch (start us, length us, event | category | flops | bytes accessed | tf_op | source)
XLA Modules:
  0.0 29.3 jit_solution(5783565961750499527)
XLA Ops:
  0.6 25.7 %step.1 = (f32[32,108]{1,0:T(8,128)}, f32[64,864]{1,0:T(8,128)}) custom-call(bf16[1,4,4,8,128]{4,3,2,1,0:T(8,128)(2,1)} %vol_h.1, bf16[32,108]{1,0:T(8,128)(2,1)} %w1_h.1, bf16[64,864]{1,0:T(8,128)(2,1)} %w2_h.1, bf16[1,64,2,4,64]{4,3,2,1,0:T(4,128)(2,1)} %cot_h.1), custom_call_target="tpu_custom_call" | custom-call | tf_op jit(solution)/shard_map/step/pallas_call | solution.py:373
  26.3 1.3 %copy.8 = f32[32,108]{1,0:T(8,128)} copy(f32[32,108]{1,0:T(8,128)} %get-tuple-element.4) | data formatting | bytes 27648
  27.6 1.6 %copy.9 = f32[64,864]{1,0:T(8,128)} copy(f32[64,864]{1,0:T(8,128)} %get-tuple-element.5) | data formatting | bytes 442368

commit v3 on v2

--- a/solution.py
+++ b/solution.py
@@ -303,16 +303,7 @@
     for x in range(wide):
         slope1[x] = slope(slope1[x])
 
-    for copy in scatter:
-        copy.wait_recv()
-    acc = jnp.zeros((rows, width), F32)
-    for i in range(n_plane):
-        acc = acc + g2r[i].astype(F32)
-    g2d[dpi] = acc.astype(BF16)
     held = lambda ref, i: (lambda r: ref.at[i])
-    across = spread(nd, dp_id, held(g2d, dpi), g2d.at[dpi], dp_send, dp_recv, 0)
-    sent += across
-
     grad1 = jnp.zeros((inner, 9 * tap_rows), F32)
     for x in range(wide):
         low = jnp.concatenate(
@@ -324,6 +315,15 @@
     g1p[me] = grad1.astype(BF16)
     firsts = spread(n_plane, plane_id, held(g1p, me), g1p.at[me], plane_send, plane_recv, 1)
     sent += firsts
+
+    for copy in scatter:
+        copy.wait_recv()
+    acc = jnp.zeros((rows, width), F32)
+    for i in range(n_plane):
+        acc = acc + g2r[i].astype(F32)
+    g2d[dpi] = acc.astype(BF16)
+    across = spread(nd, dp_id, held(g2d, dpi), g2d.at[dpi], dp_send, dp_recv, 0)
+    sent += across
 
     for copy in across:
         copy.wait_recv()
@@ -373,8 +373,8 @@
     return pl.pallas_call(
         functools.partial(kernel, nd, nx, ny),
         out_shape=(
-            jax.ShapeDtypeStruct(first_weight.shape, F32),
-            jax.ShapeDtypeStruct(second_weight.shape, F32),
+            pltpu.VMEM(first_weight.shape, F32),
+            pltpu.VMEM(second_weight.shape, F32),
         ),
         in_specs=[pl.BlockSpec(memory_space=pltpu.HBM)] * 4,
         out_specs=(vmem, vmem),
@@ -407,7 +407,7 @@
             dma((4,)),
         ],
         compiler_params=pltpu.CompilerParams(
-            collective_id=0, has_side_effects=True, vmem_limit_bytes=60 * 1024 * 1024
+            collective_id=0, has_side_effects=True, vmem_limit_bytes=57000 * 1024
         ),
         name="step",
     )(volume, first_weight, second_weight, cotangent)

time: 29.5 us -> 25.8 us (0.87)
  Pallas kernels: 25.7 us -> 23.7 us
  local copies, waits for them, and re-layouts: 2.96 us -> 1.3 us
    pallas_call x1, Pallas kernels: 25.7 us -> 23.7 us  [shards(): pl.pallas_call(functools.partial(kernel, nd, nx, ny), out_shape=(pltpu.VM...]
    unnamed x2, local copies, waits for them, and re-layouts: 2.96 us -> 1.3 us
where the time goes in v3:
time: 25.8 us; the launch traced here: 25.6 us
  Pallas kernels  23.7 us (92%)
  local copies, waits for them, and re-layouts  1.3 us (5%)
  between operations  0.64 us (2%)
    pallas_call x1, Pallas kernels, shards(): pl.pallas_call(functools.partial(kernel, nd, nx, ny), out_shape=(pltpu.VM...  23.7 us
    unnamed x2, local copies, waits for them, and re-layouts  1.3 us

profile of v3, /device:TPU:0, one launch (start us, length us, event | category | flops | bytes accessed | tf_op | source)
XLA Modules:
  0.0 25.6 jit_solution(1605989085519219889)
XLA Ops:
  0.6 23.7 %step.1 = (f32[32,108]{1,0:T(8,128)S(1)}, f32[64,864]{1,0:T(8,128)S(1)}) custom-call(bf16[1,4,4,8,128]{4,3,2,1,0:T(8,128)(2,1)} %vol_h.1, bf16[32,108]{1,0:T(8,128)(2,1)} %w1_h.1, bf16[64,864]{1,0:T(8,128)(2,1)} %w2_h.1, bf16[1,64,2,4,64]{4,3,2,1,0:T(4,128)(2,1)} %cot_h.1), custom_call_target="tpu_custom_call" | custom-call | tf_op jit(solution)/shard_map/step/pallas_call | solution.py:373
  24.3 0.6 %copy.8 = f32[32,108]{1,0:T(8,128)} copy(f32[32,108]{1,0:T(8,128)S(1)} %get-tuple-element.2) | data formatting | bytes 27648
  24.9 0.7 %copy.9 = f32[64,864]{1,0:T(8,128)} copy(f32[64,864]{1,0:T(8,128)S(1)} %get-tuple-element.3) | data formatting | bytes 442368

commit v4 on v3

--- a/solution.py
+++ b/solution.py
@@ -359,6 +359,17 @@
         copy.wait_send()
 
 
+def put_out(first, second, out1, out2, sem):
+    copies = [
+        pltpu.make_async_copy(src, dst, sem.at[i])
+        for i, (src, dst) in enumerate(((second, out2), (first, out1)))
+    ]
+    for copy in copies:
+        copy.start()
+    for copy in copies:
+        copy.wait()
+
+
 def shards(nd, nx, ny, volume, first_weight, second_weight, cotangent):
     _, chans, X, Y, Z = volume.shape
     inner, outer = first_weight.shape[0], second_weight.shape[0]
@@ -370,7 +381,7 @@
     tap_rows = -(-3 * chans // 16) * 16
     vmem = pl.BlockSpec(memory_space=pltpu.VMEM)
     dma = pltpu.SemaphoreType.DMA
-    return pl.pallas_call(
+    grads = pl.pallas_call(
         functools.partial(kernel, nd, nx, ny),
         out_shape=(
             pltpu.VMEM(first_weight.shape, F32),
@@ -411,6 +422,15 @@
         ),
         name="step",
     )(volume, first_weight, second_weight, cotangent)
+    return pl.pallas_call(
+        put_out,
+        out_shape=tuple(jax.ShapeDtypeStruct(g.shape, F32) for g in grads),
+        in_specs=[vmem] * 2,
+        out_specs=(pl.BlockSpec(memory_space=pltpu.HBM),) * 2,
+        scratch_shapes=[dma((2,))],
+        compiler_params=pltpu.CompilerParams(vmem_limit_bytes=4 * 1024 * 1024),
+        name="put_out",
+    )(*grads)
 
 
 def solution(mesh):

time: 25.8 us -> 25.2 us (0.977)
  local copies, waits for them, and re-layouts: 1.3 us -> 0 us
  Pallas kernels: 23.7 us -> 24.4 us
    unnamed x2 -> x0, local copies, waits for them, and re-layouts: 1.3 us -> none
    pallas_call x0 -> x1, Pallas kernels: none -> 0.71 us  [shards(): pl.pallas_call(put_out, out_shape=tuple((jax.ShapeDtypeStruct(g.shape, F3...]
where the time goes in v4:
time: 25.2 us; the launch traced here: 25 us
  Pallas kernels  24.4 us (97%)
  between operations  0.64 us (3%)
    pallas_call x1, Pallas kernels, shards(): pl.pallas_call(functools.partial(kernel, nd, nx, ny), out_shape=(pltpu.VM...  23.7 us
    pallas_call x1, Pallas kernels, shards(): pl.pallas_call(put_out, out_shape=tuple((jax.ShapeDtypeStruct(g.shape, F3...  0.71 us

profile of v4, /device:TPU:0, one launch (start us, length us, event | category | flops | bytes accessed | tf_op | source)
XLA Modules:
  0.0 25.0 jit_solution(12849330089721142011)
XLA Ops:
  0.6 23.7 %step.1 = (f32[32,108]{1,0:T(8,128)S(1)}, f32[64,864]{1,0:T(8,128)S(1)}) custom-call(bf16[1,4,4,8,128]{4,3,2,1,0:T(8,128)(2,1)} %vol_h.1, bf16[32,108]{1,0:T(8,128)(2,1)} %w1_h.1, bf16[64,864]{1,0:T(8,128)(2,1)} %w2_h.1, bf16[1,64,2,4,64]{4,3,2,1,0:T(4,128)(2,1)} %cot_h.1), custom_call_target="tpu_custom_call" | custom-call | tf_op jit(solution)/shard_map/step/pallas_call | solution.py:384
  24.3 0.7 %put_out.1 = (f32[32,108]{1,0:T(8,128)}, f32[64,864]{1,0:T(8,128)}) custom-call(f32[32,108]{1,0:T(8,128)S(1)} %get-tuple-element.4.first, f32[64,864]{1,0:T(8,128)S(1)} %get-tuple-element.5.second), custom_call_target="tpu_custom_call" | custom-call | tf_op jit(solution)/shard_map/put_out/pallas_call | solution.py:425
